TPU v7x, 32 devices: a whole 2x2x4 slice. The times are simulated.
32 devices in a mesh: section: 1, grp: 16 (over z, x, core), tp: 2 (over y).
Axes of the slice: x: 2, y: 2, z: 4, core: 2. Of those that a mesh axis runs over, the one named last changes fastest.
Arguments:
- partials: bfloat16 [2, 1, 2048, 8192], P('tp', 'section', 'grp'), may hold values from -3 to 3
- residual: bfloat16 [1, 2048, 8192], P('section', 'grp', 'tp'), may hold values from -300 to 300
- norm_gain: bfloat16 [8192], replicated, may hold values from 0.099609375 to 1.8984375
- w_query: bfloat16 [8192, 8192], P('grp', ('section', 'tp')), may hold values from -0.0625 to 0.0625
- w_keyval: bfloat16 [8192, 2048], P('grp', ('section', 'tp')), may hold values from -0.0625 to 0.0625
- bias_query: bfloat16 [8192], P(('section', 'tp')), may hold values from -3 to 3
- bias_keyval: bfloat16 [2048], P(('section', 'tp')), may hold values from -3 to 3
Outputs:
- hidden: bfloat16 [1, 2048, 8192], P('section', 'grp', 'tp')
- query: bfloat16 [1, 2048, 8192], P(None, 'grp', ('section', 'tp'))
- keyval: bfloat16 [1, 2048, 2048], P(None, 'grp', ('section', 'tp'))
All inputs are finite; a program needn't handle non-finite values.
Results may differ from a plain program's by a relative error of at most 0.01.
Values may be sent and summed in bfloat16 or wider, within the bound.
A program may use at most 192 MiB of HBM per device.

v0:
```python
import jax
import jax.numpy as jnp
from jax import lax
from jax.sharding import PartitionSpec as P

epsilon = 1e-06


def local(partials, residual, norm_gain, w_query, w_keyval, bias_query, bias_keyval):
    model_width = norm_gain.shape[0]
    summed = lax.psum_scatter(partials[0], "tp", scatter_dimension=2, tiled=True).astype(
        jnp.float32
    )
    hidden = (residual.astype(jnp.float32) + summed).astype(jnp.bfloat16)
    widened = hidden.astype(jnp.float32)
    squares = lax.psum(jnp.sum(widened * widened, axis=-1), "tp")
    feature_share = widened.shape[2]
    offset = lax.axis_index("tp") * feature_share
    local_gain = lax.dynamic_slice_in_dim(norm_gain, offset, feature_share, 0).astype(jnp.float32)
    scaled = (widened * local_gain).astype(jnp.bfloat16)
    scaled = lax.all_gather(scaled, "tp", axis=2, tiled=True)
    gathered_squares = lax.all_gather(squares, "section", axis=0, tiled=True)
    scale = lax.rsqrt(gathered_squares / model_width + epsilon)[..., None]
    exchanged = lax.all_to_all(scaled, "grp", split_axis=2, concat_axis=1, tiled=True)
    exchanged = lax.all_gather(exchanged, "section", axis=0, tiled=True)
    seqs, length, depth = exchanged.shape
    flat = exchanged.reshape(seqs * length, depth)

    def project(weight, bias):
        total = jnp.dot(flat, weight, preferred_element_type=jnp.float32).astype(jnp.bfloat16)
        total = total.reshape(seqs, length, -1)
        own = lax.psum_scatter(total, "grp", scatter_dimension=1, tiled=True)
        return (own.astype(jnp.float32) * scale + bias.astype(jnp.float32)).astype(jnp.bfloat16)

    keyval = project(w_keyval, bias_keyval)
    query = project(w_query, bias_query)
    return (hidden, query, keyval)


def solution(mesh):
    placed = (
        P("tp", "section", "grp", None),
        P("section", "grp", "tp"),
        P(),
        P("grp", ("section", "tp")),
        P("grp", ("section", "tp")),
        P(("section", "tp")),
        P(("section", "tp")),
    )
    return jax.shard_map(
        local,
        mesh=mesh,
        in_specs=placed,
        out_specs=(
            P("section", "grp", "tp"),
            P(None, "grp", ("section", "tp")),
            P(None, "grp", ("section", "tp")),
        ),
        check_vma=False,
    )
```

profile of v0, /device:TPU:0, one launch (start us, length us, event | category | flops | bytes accessed | tf_op | source)
XLA Modules:
  0.0 471.7 jit_solution(13430152191114884679)
XLA Ops:
  7.2 0.0 copy-start
  7.2 0.0 copy-start.5
  7.2 0.0 copy-start.3
  7.2 0.0 reduce-scatter.4.cloned.1.call-start
  7.2 0.7 reduce-scatter.4.cloned.1.call-update
  7.9 0.0 all-gather.2.cloned.1.call-start
  8.0 0.0 copy-done.5
  8.0 36.9 %reduce-scatter.4.cloned.1.call-done = bf16[1,128,4096]{2,1,0:T(8,128)(2,1)} async-done(((bf16[1,128,8192]{2,1,0:T(8,128)(2,1)}), bf16[1,128,4096]{2,1,0:T(8,128)(2,1)}) %reduce-scatter.4.cloned.1.call-update) | async-done | bytes 1048592 | tf_op jit(solution)/shard_map/reduce_scatter | solution.py:11
  44.9 0.0 copy-done.3
  44.9 1.7 fusion.1
  46.6 0.0 copy-start.1
  46.6 1.0 copy-done.1
  47.6 1.2 fusion
  48.7 0.0 all-gather.2.cloned.1.call-update
  48.8 0.0 reduce-scatter.8.cloned.1.call-start
  48.8 33.2 %all-gather.2.cloned.1.call-done = bf16[1,128,8192]{2,1,0:T(8,128)(2,1)} async-done(((bf16[1,128,4096]{2,1,0:T(8,128)(2,1)}), bf16[1,128,8192]{2,1,0:T(8,128)(2,1)}) %all-gather.2.cloned.1.call-update) | async-done | bytes 2097168 | tf_op jit(solution)/shard_map/all_gather | solution.py:21
  82.0 9.5 %copy.18 = bf16[1,128,8192]{1,0,2:T(2,128)(2,1)} copy(bf16[1,128,8192]{2,1,0:T(8,128)(2,1)} %all-gather.2.cloned.1.call-done) | data formatting | bytes 4194304 | tf_op jit(solution)/shard_map/all_gather | solution.py:21
  91.5 0.5 broadcast.9
  92.0 45.2 %reduce.1 = bf16[8192,128]{1,0:T(8,128)(2,1)S(1)} reduce(bf16[8192,1,128]{2,1,0:T(2,128)(2,1)} %bitcast.18, bf16[]{:T(256)} %broadcast.9), dimensions={1}, to_apply=%bitcast.12.reduce_sub_computation | reduce | bytes 4194306
  137.2 2.1 reshape.33
  139.3 52.8 %all_to_all.15 = bf16[16,2,32768]{2,1,0:T(2,128)(2,1)S(1)} all-to-all(bf16[16,2,32768]{2,1,0:T(2,128)(2,1)} %reshape.33), channel_id=1, replica_groups=mesh['section'=1,'grp'=16,'tp'=2] {'grp'}, dimensions={0} | all-to-all | bytes 4194304 | tf_op jit(solution)/shard_map/all_to_all | solution.py:24
  192.0 6.8 %reshape.34 = bf16[8192,1,128]{2,1,0:T(2,128)(2,1)} reshape(bf16[16,2,32768]{2,1,0:T(2,128)(2,1)S(1)} %all_to_all.15) | data formatting | bytes 4194304
  198.8 2.5 copy.20
  201.3 2.6 copy.19
  203.9 0.0 copy-done
  203.9 5.9 %convert_bitcast_fusion.1 = bf16[1,2048,1024]{2,1,0:T(8,128)(2,1)} fusion(bf16[2048,512]{1,0:T(8,128)(2,1)} %bitcast.22, bf16[512,1024]{1,0:T(8,128)(2,1)S(1)} %copy-done), kind=kOutput, calls=%fused_computation.1 | convolution fusion | flops 2149580800 | bytes 7340032 | tf_op jit(solution)/shard_map/dot_general | solution.py:30
  209.8 0.0 copy-start.2
  209.8 0.0 reduce-scatter.8.cloned.1.call-update
  209.8 0.2 reduce-scatter.6.cloned.1.call-start
  210.0 1.3 copy-done.2
  211.3 13.8 %convert_bitcast_fusion = bf16[1,2048,4096]{2,1,0:T(8,128)(2,1)} fusion(bf16[2048,512]{1,0:T(8,128)(2,1)S(1)} %bitcast.23, bf16[512,4096]{1,0:T(8,128)(2,1)} %param.10), kind=kOutput, calls=%fused_computation | convolution fusion | flops 8598323200 | bytes 23068672 | tf_op jit(solution)/shard_map/dot_general | solution.py:30
  225.2 0.0 copy-start.6
  225.2 0.0 copy-start.4
  225.2 0.0 reduce-scatter.6.cloned.1.call-update
  225.2 0.7 copy-done.6
  225.9 0.0 copy-done.4
  225.9 4.9 %psum.7 = f32[1,128]{1,0:T(1,128)S(1)} all-reduce(f32[1,128]{1,0:T(1,128)S(1)} %bitcast.24), channel_id=1, replica_groups=mesh['section'=1,'grp'=16,'tp'=2] {'tp'}, use_global_device_ids=true, to_apply=%region_3.0 | all-reduce | flops 128 | bytes 1024 | tf_op jit(solution)/shard_map/psum | solution.py:16
  230.9 51.4 %reduce-scatter.8.cloned.1.call-done = bf16[1,128,1024]{2,1,0:T(8,128)(2,1)} async-done(((bf16[1,2048,1024]{2,1,0:T(8,128)(2,1)}), bf16[1,128,1024]{2,1,0:T(8,128)(2,1)}) %reduce-scatter.8.cloned.1.call-update) | async-done | bytes 262160 | tf_op jit(solution)/shard_map/reduce_scatter | solution.py:32
  282.3 1.8 add_convert_fusion.2
  284.1 178.6 %reduce-scatter.6.cloned.1.call-done = bf16[1,128,4096]{2,1,0:T(8,128)(2,1)} async-done(((bf16[1,2048,4096]{2,1,0:T(8,128)(2,1)}), bf16[1,128,4096]{2,1,0:T(8,128)(2,1)}) %reduce-scatter.6.cloned.1.call-update) | async-done | bytes 1048592 | tf_op jit(solution)/shard_map/reduce_scatter | solution.py:32
  462.6 2.5 add_convert_fusion
  (4 shorter events, 0.0 us)
Async XLA Ops:
  7.2 196.7 %copy-start = (bf16[512,1024]{1,0:T(8,128)(2,1)S(1)}, bf16[512,1024]{1,0:T(8,128)(2,1)}, u32[]{:S(2)}) copy-start(bf16[512,1024]{1,0:T(8,128)(2,1)} %param.11) | copy-start | bytes 3145732
  7.2 0.8 copy-start.5
  7.2 37.7 %copy-start.3 = (bf16[1,128,4096]{2,1,0:T(8,128)(2,1)S(1)}, bf16[1,128,4096]{2,1,0:T(8,128)(2,1)}, u32[]{:S(2)}) copy-start(bf16[1,128,4096]{2,1,0:T(8,128)(2,1)} %param.8) | copy-start | bytes 3145732
  7.2 37.7 %reduce-scatter.4.cloned.1.call-start = ((), (), s32[]{:S(2)}) async-start(), calls=%async_computation.4 | async-start | bytes 3145728 | tf_op jit(solution)/shard_map/reduce_scatter | solution.py:11
  7.9 74.1 %all-gather.2.cloned.1.call-start = ((), (), s32[]{:S(2)}) async-start(), calls=%async_computation.5 | async-start | bytes 3145728 | tf_op jit(solution)/shard_map/all_gather | solution.py:21
  46.6 1.0 copy-start.1
  48.8 233.5 %reduce-scatter.8.cloned.1.call-start = ((), (), s32[]{:S(2)}) async-start(), calls=%async_computation.7 | async-start | bytes 4456448 | tf_op jit(solution)/shard_map/reduce_scatter | solution.py:32
  209.8 1.6 copy-start.2
  209.8 252.9 %reduce-scatter.6.cloned.1.call-start = ((), (), s32[]{:S(2)}) async-start(), calls=%async_computation.6 | async-start | bytes 17825792 | tf_op jit(solution)/shard_map/reduce_scatter | solution.py:32
  225.2 0.7 copy-start.6
  225.2 0.7 copy-start.4
Sparse Core Ops, SparseCore 0:
  10.2 34.6 reduce-scatter.3
  48.9 33.0 all-gather.1
  209.9 72.3 reduce-scatter.7
  286.3 176.3 reduce-scatter.5
where the time goes:
time: 472 us
  waiting for transfers between devices  301 us (64%)
  blocking collectives  57.7 us (12%)
  other arithmetic  52.3 us (11%)
  local copies, waits for them, and re-layouts  26.9 us (6%)
  matrix products  19.7 us (4%)
  between operations  13.8 us (3%)
    reduce_scatter x2, waiting for transfers between devices, project(): own = lax.psum_scatter(total, 'grp', scatter_dimension=1, tiled=True)  230 us
    all_to_all x1, blocking collectives, local(): lax.all_to_all(scaled, 'grp', split_axis=2, concat_axis=1, tiled=True)  52.8 us
    unnamed x1, other arithmetic  45.2 us
    reduce_scatter x1, waiting for transfers between devices, local(): lax.psum_scatter(partials[0], 'tp', scatter_dimension=2, tiled=True)  36.9 us
    all_gather x1, waiting for transfers between devices, local(): scaled = lax.all_gather(scaled, 'tp', axis=2, tiled=True)  33.2 us
    dot_general x2, matrix products, project(): jnp.dot(flat, weight, preferred_element_type=jnp.float32)  19.7 us
    unnamed x18, local copies, waits for them, and re-layouts  14.8 us
    all_gather x1, local copies, waits for them, and re-layouts, local(): scaled = lax.all_gather(scaled, 'tp', axis=2, tiled=True)  9.49 us
  transfers between devices with their start and end apart: 4, of which 4 were waited for; matrix products, arithmetic and copies ran while one was open for 3% of the time, Pallas kernels for 0%

commit v1 on v0

--- a/solution.py
+++ b/solution.py
@@ -21,7 +21,15 @@
     scaled = lax.all_gather(scaled, "tp", axis=2, tiled=True)
     gathered_squares = lax.all_gather(squares, "section", axis=0, tiled=True)
     scale = lax.rsqrt(gathered_squares / model_width + epsilon)[..., None]
-    exchanged = lax.all_to_all(scaled, "grp", split_axis=2, concat_axis=1, tiled=True)
+    exchanged = jnp.concatenate(
+        lax.all_to_all(
+            jnp.stack(jnp.split(scaled, lax.axis_size("grp"), axis=2)),
+            axis_name="grp",
+            split_axis=0,
+            concat_axis=0,
+        ),
+        axis=1,
+    )
     exchanged = lax.all_gather(exchanged, "section", axis=0, tiled=True)
     seqs, length, depth = exchanged.shape
     flat = exchanged.reshape(seqs * length, depth)

time: 472 us -> 415 us (0.88)
  other arithmetic: 52.3 us -> 7.32 us
  local copies, waits for them, and re-layouts: 26.9 us -> 15.4 us
    unnamed x1 -> x0, other arithmetic: 45.2 us -> none
    all_gather x1 -> x0, local copies, waits for them, and re-layouts: 9.49 us -> none  [local(): scaled = lax.all_gather(scaled, 'tp', axis=2, tiled=True)]
    unnamed x18 -> x27, local copies, waits for them, and re-layouts: 14.8 us -> 14.4 us
  transfers between devices with their start and end apart: 4 -> 4, of which waited for: 4 -> 4; matrix products, arithmetic and copies ran while one was open for 3% -> 4% of each run, Pallas kernels for 0% -> 0%
where the time goes in v1:
time: 415 us
  waiting for transfers between devices  302 us (73%)
  blocking collectives  57.5 us (14%)
  matrix products  18.1 us (4%)
  local copies, waits for them, and re-layouts  15.4 us (4%)
  between operations  13.9 us (3%)
  other arithmetic  7.32 us (2%)
    reduce_scatter x2, waiting for transfers between devices, project(): own = lax.psum_scatter(total, 'grp', scatter_dimension=1, tiled=True)  232 us
    all_to_all x1, blocking collectives, local(): lax.all_to_all(jnp.stack(jnp.split(scaled, lax.axis_size('grp'), axis=2))...  52.6 us
    reduce_scatter x1, waiting for transfers between devices, local(): lax.psum_scatter(partials[0], 'tp', scatter_dimension=2, tiled=True)  36.9 us
    all_gather x1, waiting for transfers between devices, local(): scaled = lax.all_gather(scaled, 'tp', axis=2, tiled=True)  33.2 us
    dot_general x2, matrix products, project(): jnp.dot(flat, weight, preferred_element_type=jnp.float32)  18.1 us
    unnamed x27, local copies, waits for them, and re-layouts  14.4 us
  transfers between devices with their start and end apart: 4, of which 4 were waited for; matrix products, arithmetic and copies ran while one was open for 4% of the time, Pallas kernels for 0%

profile of v1, /device:TPU:0, one launch (start us, length us, event | category | flops | bytes accessed | tf_op | source)
XLA Modules:
  0.0 414.7 jit_solution(8445795867458336674)
XLA Ops:
  7.2 0.0 copy-start
  7.2 0.0 copy-start.4
  7.2 0.0 copy-start.2
  7.2 0.0 reduce-scatter.4.cloned.1.call-start
  7.2 0.7 reduce-scatter.4.cloned.1.call-update
  7.9 0.0 all-gather.2.cloned.1.call-start
  8.0 0.0 copy-done.4
  8.0 36.9 %reduce-scatter.4.cloned.1.call-done = bf16[1,128,4096]{2,1,0:T(8,128)(2,1)} async-done(((bf16[1,128,8192]{2,1,0:T(8,128)(2,1)}), bf16[1,128,4096]{2,1,0:T(8,128)(2,1)}) %reduce-scatter.4.cloned.1.call-update) | async-done | bytes 1048592 | tf_op jit(solution)/shard_map/reduce_scatter | solution.py:11
  44.9 0.0 copy-done.2
  44.9 1.7 fusion.1
  46.6 0.0 copy-start.1
  46.6 1.3 fusion
  47.9 0.0 all-gather.2.cloned.1.call-update
  47.9 0.0 reduce-scatter.8.cloned.1.call-start
  48.0 33.2 %all-gather.2.cloned.1.call-done = bf16[1,128,8192]{2,1,0:T(8,128)(2,1)} async-done(((bf16[1,128,4096]{2,1,0:T(8,128)(2,1)}), bf16[1,128,8192]{2,1,0:T(8,128)(2,1)}) %all-gather.2.cloned.1.call-update) | async-done | bytes 2097168 | tf_op jit(solution)/shard_map/all_gather | solution.py:21
  81.2 0.9 fusion.17
  82.1 0.9 fusion.16
  83.0 0.9 fusion.15
  83.9 0.9 fusion.14
  84.9 0.0 copy-done.1
  84.9 0.9 fusion.13
  85.8 0.9 fusion.12
  86.7 0.9 fusion.11
  87.6 0.9 fusion.10
  88.6 0.9 fusion.9
  89.5 0.9 fusion.8
  90.4 0.9 fusion.7
  91.3 0.9 fusion.6
  92.2 0.9 fusion.5
  93.1 0.9 fusion.4
  94.1 0.9 fusion.3
  95.0 0.9 fusion.2
  95.9 52.6 %all_to_all.5 = bf16[16,1,128,512]{3,2,1,0:T(8,128)(2,1)S(1)} all-to-all(bf16[16,1,128,512]{3,2,1,0:T(8,128)(2,1)S(1)} %fusion.2), channel_id=1, replica_groups=mesh['section'=1,'grp'=16,'tp'=2] {'grp'}, dimensions={0} | all-to-all | bytes 4194304 | tf_op jit(solution)/shard_map/all_to_all | solution.py:25
  148.5 0.0 copy-done
  148.5 4.3 %convert_bitcast_fusion.1 = bf16[1,2048,1024]{2,1,0:T(8,128)(2,1)} fusion(bf16[2048,512]{1,0:T(8,128)(2,1)S(1)} %bitcast.78, bf16[512,1024]{1,0:T(8,128)(2,1)S(1)} %copy-done), kind=kOutput, calls=%fused_computation.1 | convolution fusion | flops 2149580800 | bytes 7340032 | tf_op jit(solution)/shard_map/dot_general | solution.py:38
  152.7 0.0 reduce-scatter.8.cloned.1.call-update
  152.8 0.0 reduce-scatter.6.cloned.1.call-start
  152.8 13.9 %convert_bitcast_fusion = bf16[1,2048,4096]{2,1,0:T(8,128)(2,1)} fusion(bf16[2048,512]{1,0:T(8,128)(2,1)S(1)} %bitcast.79, bf16[512,4096]{1,0:T(8,128)(2,1)} %param.10), kind=kOutput, calls=%fused_computation | convolution fusion | flops 8598323200 | bytes 23068672 | tf_op jit(solution)/shard_map/dot_general | solution.py:38
  166.7 0.0 copy-start.5
  166.7 0.0 copy-start.3
  166.7 0.0 reduce-scatter.6.cloned.1.call-update
  166.7 0.7 copy-done.5
  167.4 0.0 copy-done.3
  167.4 4.9 %psum.7 = f32[1,128]{1,0:T(1,128)S(1)} all-reduce(f32[1,128]{1,0:T(1,128)S(1)} %bitcast.80), channel_id=1, replica_groups=mesh['section'=1,'grp'=16,'tp'=2] {'tp'}, use_global_device_ids=true, to_apply=%region_3.0 | all-reduce | flops 128 | bytes 1024 | tf_op jit(solution)/shard_map/psum | solution.py:16
  172.4 52.9 %reduce-scatter.8.cloned.1.call-done = bf16[1,128,1024]{2,1,0:T(8,128)(2,1)} async-done(((bf16[1,2048,1024]{2,1,0:T(8,128)(2,1)}), bf16[1,128,1024]{2,1,0:T(8,128)(2,1)}) %reduce-scatter.8.cloned.1.call-update) | async-done | bytes 262160 | tf_op jit(solution)/shard_map/reduce_scatter | solution.py:40
  225.3 1.8 add_convert_fusion.2
  227.1 178.6 %reduce-scatter.6.cloned.1.call-done = bf16[1,128,4096]{2,1,0:T(8,128)(2,1)} async-done(((bf16[1,2048,4096]{2,1,0:T(8,128)(2,1)}), bf16[1,128,4096]{2,1,0:T(8,128)(2,1)}) %reduce-scatter.6.cloned.1.call-update) | async-done | bytes 1048592 | tf_op jit(solution)/shard_map/reduce_scatter | solution.py:40
  405.7 2.5 add_convert_fusion
  (4 shorter events, 0.0 us)
Async XLA Ops:
  7.2 141.3 %copy-start = (bf16[512,1024]{1,0:T(8,128)(2,1)S(1)}, bf16[512,1024]{1,0:T(8,128)(2,1)}, u32[]{:S(2)}) copy-start(bf16[512,1024]{1,0:T(8,128)(2,1)} %param.11) | copy-start | bytes 3145732
  7.2 0.8 copy-start.4
  7.2 37.7 %copy-start.2 = (bf16[1,128,4096]{2,1,0:T(8,128)(2,1)S(1)}, bf16[1,128,4096]{2,1,0:T(8,128)(2,1)}, u32[]{:S(2)}) copy-start(bf16[1,128,4096]{2,1,0:T(8,128)(2,1)} %param.8) | copy-start | bytes 3145732
  7.2 37.7 %reduce-scatter.4.cloned.1.call-start = ((), (), s32[]{:S(2)}) async-start(), calls=%async_computation.4 | async-start | bytes 3145728 | tf_op jit(solution)/shard_map/reduce_scatter | solution.py:11
  7.9 73.3 %all-gather.2.cloned.1.call-start = ((), (), s32[]{:S(2)}) async-start(), calls=%async_computation.5 | async-start | bytes 3145728 | tf_op jit(solution)/shard_map/all_gather | solution.py:21
  46.6 38.3 %copy-start.1 = (bf16[1,128,4096]{2,1,0:T(8,128)(2,1)}, bf16[1,128,4096]{2,1,0:T(8,128)(2,1)S(1)}, u32[]{:S(2)}) copy-start(bf16[1,128,4096]{2,1,0:T(8,128)(2,1)S(1)} %get-tuple-element.4) | copy-start | bytes 3145732
  47.9 177.3 %reduce-scatter.8.cloned.1.call-start = ((), (), s32[]{:S(2)}) async-start(), calls=%async_computation.7 | async-start | bytes 4456448 | tf_op jit(solution)/shard_map/reduce_scatter | solution.py:40
  152.8 252.9 %reduce-scatter.6.cloned.1.call-start = ((), (), s32[]{:S(2)}) async-start(), calls=%async_computation.6 | async-start | bytes 17825792 | tf_op jit(solution)/shard_map/reduce_scatter | solution.py:40
  166.7 0.7 copy-start.5
  166.7 0.7 copy-start.3
Sparse Core Ops, SparseCore 0:
  10.2 34.6 reduce-scatter.3
  48.1 33.0 all-gather.1
  152.9 72.3 reduce-scatter.7
  229.2 176.3 reduce-scatter.5
